TPU v7x, 32 devices: a whole 2x2x4 slice. The times are simulated.
32 devices in a mesh: pa: 32 (over z, y, x, core).
Axes of the slice: x: 2, y: 2, z: 4, core: 2. Of those that a mesh axis runs over, the one named last changes fastest.
Arguments:
- image_real: float32 [8, 4096, 4096], P(None, 'pa'), may hold values from -6 to 6
- image_imag: float32 [8, 4096, 4096], P(None, 'pa'), may hold values from -6 to 6
Outputs:
- spectrum_real: float32 [8, 4096, 4096], P(None, 'pa')
- spectrum_imag: float32 [8, 4096, 4096], P(None, 'pa')
All inputs are finite; a program needn't handle non-finite values.
Results may differ from a plain program's by a relative error of at most 0.0003.
Values sent between devices are 32-bit elements.
A program may use at most 256 MiB of HBM per device.

v0:
```python
import math

import jax
import jax.numpy as jnp
from jax import lax
from jax.sharding import PartitionSpec as P

SPLIT_A = 64


canceller_gain = 1.0 / math.sqrt(6.0)


def hamming(offset, sample_count, length):
    sample_index = (offset + jnp.arange(sample_count, dtype=jnp.int32)).astype(jnp.float32)
    return 0.54 - 0.46 * jnp.cos(sample_index * (2.0 * math.pi / length))


def cancel_along(extended, time_axis):
    extent = extended.shape[time_axis]
    newest = lax.slice_in_dim(extended, 2, extent, axis=time_axis)
    middle = lax.slice_in_dim(extended, 1, extent - 1, axis=time_axis)
    oldest = lax.slice_in_dim(extended, 0, extent - 2, axis=time_axis)
    return (newest - 2.0 * middle + oldest) * canceller_gain


def twiddle(row_count, col_count, length):
    product = (
        jnp.arange(row_count, dtype=jnp.int32)[:, None]
        * jnp.arange(col_count, dtype=jnp.int32)[None, :]
        % length
    )
    angles = product.astype(jnp.float32) * (-2.0 * math.pi / length)
    return (jnp.cos(angles), jnp.sin(angles))


def block_matrix(extent):
    cosine_part, sine_part = twiddle(extent, extent, extent)
    return jnp.stack([jnp.stack([cosine_part, -sine_part]), jnp.stack([sine_part, cosine_part])])


def transform_last(stacked, transposed):
    planes, frame_count, middle, length = stacked.shape
    first_size = SPLIT_A
    second_size = length // first_size
    tiled = stacked.reshape(planes, frame_count, middle, first_size, second_size)
    section_one = jnp.einsum(
        "cdki,dfmij->cfmkj",
        block_matrix(first_size),
        tiled,
        precision=lax.Precision.HIGHEST,
        preferred_element_type=jnp.float32,
    )
    twiddle_real, twiddle_imag = twiddle(first_size, second_size, length)
    turned = jnp.stack(
        [
            section_one[0] * twiddle_real - section_one[1] * twiddle_imag,
            section_one[0] * twiddle_imag + section_one[1] * twiddle_real,
        ]
    )
    if transposed:
        section_two = jnp.einsum(
            "cdlj,dfmkj->cflkm",
            block_matrix(second_size),
            turned,
            precision=lax.Precision.HIGHEST,
            preferred_element_type=jnp.float32,
        )
        return section_two.reshape(planes, frame_count, length, middle)
    section_two = jnp.einsum(
        "cdlj,dfmkj->cfmlk",
        block_matrix(second_size),
        turned,
        precision=lax.Precision.HIGHEST,
        preferred_element_type=jnp.float32,
    )
    return section_two.reshape(planes, frame_count, middle, length)


def redistribute(spectrum):
    return lax.all_to_all(spectrum, "pa", split_axis=2, concat_axis=3, tiled=True)


def body(image_real, image_imag):
    frame_count, row_count, length = image_real.shape
    stacked = jnp.stack([image_real, image_imag])
    col_window = hamming(0, length, length)
    columns = redistribute(transform_last(stacked * col_window, True))
    padded = jnp.pad(columns, ((0, 0), (0, 0), (0, 0), (2, 0)))
    columns = cancel_along(padded, 3) * col_window
    finished = transform_last(columns, False) * (1.0 / length)
    return (finished[0], finished[1])


def solution(mesh):
    placed = (P(None, "pa", None), P(None, "pa", None))
    return jax.shard_map(
        body,
        mesh=mesh,
        in_specs=placed,
        out_specs=(P(None, "pa", None), P(None, "pa", None)),
        check_vma=False,
    )
```

profile of v0, /device:TPU:5, one launch (start us, length us, event | category | flops | bytes accessed | tf_op | source)
XLA Modules:
  0.0 1336.2 jit_solution(10533249913423667814)
XLA Ops:
  0.6 0.1 fusion.35
  0.8 0.1 fusion.37
  0.9 0.1 multiply_subtract_fusion.2
  1.1 0.1 fusion.33
  1.2 0.0 copy-start
  1.2 0.0 copy-start.2
  1.2 17.4 %copy.32 = f32[8,128,4096]{1,2,0:T(8,128)} copy(f32[8,128,4096]{2,1,0:T(8,128)} %param.2) | data formatting | bytes 33554432 | tf_op args[0]
  18.7 17.4 %copy.33 = f32[8,128,4096]{1,2,0:T(8,128)} copy(f32[8,128,4096]{2,1,0:T(8,128)} %param.3) | data formatting | bytes 33554432 | tf_op args[1]
  36.1 13.1 fusion
  49.3 62.6 %fusion.12 = f32[2,8,128,64,64]{2,3,0,4,1:T(8,128)} fusion(f32[2,8,128,64,64,1]{2,4,3,1,0,5:T(8,128)S(1)} %fusion, f32[1,2,64,64]{3,2,1,0:T(8,128)S(1)} %get-tuple-element.15, f32[1,2,64,64]{3,2,1,0:T(8,128)S(1)} %get-tuple-element.14), kind=kOutput, calls=%fused_computation.19 | convolution fusion | flops 12884918272 | bytes 67174400 | tf_op jit(solution)/shard_map/cdki,dfmij->cfmkj/dot_general | solution.py:47
  111.8 0.0 copy-done
  111.8 0.0 copy-done.2
  111.8 22.9 %multiply_subtract_fusion.1 = (f32[1,8,128,64,64]{2,3,0,4,1:T(8,128)}, f32[1,8,128,64,64]{2,3,0,4,1:T(8,128)}) fusion(f32[2,8,128,64,64]{2,3,0,4,1:T(8,128)} %fusion.12, f32[64,64]{0,1:T(8,128)S(1)} %get-tuple-element.18, f32[64,64]{0,1:T(8,128)S(1)} %get-tuple-element.19), kind=kLoop, calls=%fused_computation.18 | loop fusion | flops 25165824 | bytes 67141632 | tf_op jit(solution)/shard_map/sub | solution.py:57
  134.7 12.9 maximum_bitcast_fusion
  147.6 63.2 %fusion.15 = f32[2,8,64,64,128]{4,2,0,3,1:T(8,128)} fusion(f32[2,8,128,64,64,1]{2,3,0,4,1,5:T(8,128)S(1)} %maximum_bitcast_fusion, f32[1,2,64,64]{3,2,1,0:T(8,128)S(1)} %get-tuple-element.15, f32[1,2,64,64]{3,2,1,0:T(8,128)S(1)} %get-tuple-element.14), kind=kOutput, calls=%fused_computation.20 | convolution fusion | flops 12884918272 | bytes 67174400 | tf_op jit(solution)/shard_map/cdlj,dfmkj->cflkm/dot_general | solution.py:62
  210.8 28.3 %copy.36 = f32[2,8,64,64,128]{4,3,2,1,0:T(8,128)S(1)} copy(f32[2,8,64,64,128]{4,2,0,3,1:T(8,128)} %fusion.15) | data formatting | bytes 67108864 | tf_op jit(solution)/shard_map/cdlj,dfmkj->cflkm/transpose | solution.py:62
  239.1 42.9 %copy.37 = f32[2,8,4096,128]{3,1,0,2:T(8,128)} copy(f32[2,8,4096,128]{3,2,1,0:T(8,128)S(1)} %bitcast.64) | data formatting | bytes 67108864 | tf_op jit(solution)/shard_map/reshape | solution.py:69
  282.0 6.8 all-to-all-start
  288.8 0.1 subtract_multiply_fusion
  288.9 734.0 %all-to-all-done = f32[2,8,4096,128]{3,1,0,2:T(8,128)} async-done(((f32[2,8,4096,128]{3,1,0,2:T(8,128)}), f32[2,8,4096,128]{3,1,0,2:T(8,128)}, u32[]{:S(2)}, u32[]{:S(2)}) %all-to-all-start) | async-done | bytes 33554464 | tf_op jit(solution)/shard_map/all_to_all | solution.py:81
  1022.9 31.1 %copy.39 = f32[2,8,128,32,128]{2,4,3,1,0:T(8,128)} copy(f32[2,8,128,32,128]{4,1,0,2,3:T(8,128)} %bitcast.18) | data formatting | bytes 67108864 | tf_op jit(solution)/shard_map/all_to_all | solution.py:81
  1054.0 44.2 %add_multiply_fusion = f32[2,8,128,4096]{2,3,1,0:T(8,128)} fusion(f32[2,8,128,4096]{2,3,1,0:T(8,128)} %bitcast.62, f32[4096]{0:T(1024)S(1)} %subtract_multiply_fusion), kind=kLoop, calls=%fused_computation.14 | loop fusion | flops 33554432 | bytes 67125248 | tf_op jit(solution)/shard_map/mul | solution.py:90
  1098.2 57.5 %fusion.18 = f32[2,8,128,64,64]{2,3,0,4,1:T(8,128)} fusion(f32[2,8,128,64,64,1]{2,4,3,1,0,5:T(8,128)} %bitcast.63, f32[1,2,64,64]{3,2,1,0:T(8,128)S(1)} %get-tuple-element.15, f32[1,2,64,64]{3,2,1,0:T(8,128)S(1)} %get-tuple-element.14), kind=kOutput, calls=%fused_computation.21 | convolution fusion | flops 12884918272 | bytes 67174400 | tf_op jit(solution)/shard_map/cdki,dfmij->cfmkj/dot_general | solution.py:47
  1155.7 0.0 copy-done.1
  1155.7 22.9 %multiply_subtract_fusion = (f32[1,8,128,64,64]{2,3,0,4,1:T(8,128)}, f32[1,8,128,64,64]{2,3,0,4,1:T(8,128)}) fusion(f32[2,8,128,64,64]{2,3,0,4,1:T(8,128)} %fusion.18, f32[64,64]{0,1:T(8,128)S(1)} %copy-done.1, f32[64,64]{0,1:T(8,128)S(1)} %copy-done.3), kind=kLoop, calls=%fused_computation.16 | loop fusion | flops 25165824 | bytes 67141632 | tf_op jit(solution)/shard_map/sub | solution.py:57
  1178.6 12.9 maximum_bitcast_fusion.1
  1191.4 63.2 %fusion.1 = f32[2,8,128,64,64]{2,3,0,4,1:T(8,128)} fusion(f32[2,8,128,64,64,1]{2,3,0,4,1,5:T(8,128)S(1)} %maximum_bitcast_fusion.1, f32[1,2,64,64]{3,2,1,0:T(8,128)S(1)} %get-tuple-element.15, f32[1,2,64,64]{3,2,1,0:T(8,128)S(1)} %get-tuple-element.14), kind=kOutput, calls=%fused_computation.5 | convolution fusion | flops 12893306880 | bytes 67174400 | tf_op jit(solution)/shard_map/cdlj,dfmkj->cfmlk/dot_general | solution.py:70
  1254.6 17.1 %fusion.42 = (f32[1,8,128,64,64]{2,3,0,4,1:T(8,128)}, f32[1,8,128,64,64]{2,3,0,4,1:T(8,128)S(1)}) fusion(f32[2,8,128,64,64]{2,3,0,4,1:T(8,128)} %fusion.1), kind=kLoop, calls=%fused_computation.54 | loop fusion | bytes 67108864 | tf_op jit(solution)/shard_map/slice | solution.py:92
  1271.7 11.7 copy.42
  1283.4 17.5 %copy.44 = f32[8,128,4096]{2,1,0:T(8,128)} copy(f32[8,128,4096]{1,2,0:T(8,128)} %bitcast.65) | data formatting | bytes 33554432
  1300.9 17.7 %copy.43 = f32[1,8,128,64,64]{2,4,3,1,0:T(8,128)} copy(f32[1,8,128,64,64]{2,3,0,4,1:T(8,128)} %get-tuple-element.12) | data formatting | bytes 33554432 | tf_op jit(solution)/shard_map/slice | solution.py:92
  1318.5 17.5 %copy.45 = f32[8,128,4096]{2,1,0:T(8,128)} copy(f32[8,128,4096]{1,2,0:T(8,128)} %bitcast.66) | data formatting | bytes 33554432
  (4 shorter events, 0.0 us)
Async XLA Ops:
  1.2 110.6 %copy-start = (f32[64,64]{0,1:T(8,128)}, f32[64,64]{0,1:T(8,128)S(1)}, u32[]{:S(2)}) copy-start(f32[64,64]{0,1:T(8,128)S(1)} %get-tuple-element.18) | copy-start | bytes 49156
  1.2 110.6 %copy-start.2 = (f32[64,64]{0,1:T(8,128)}, f32[64,64]{0,1:T(8,128)S(1)}, u32[]{:S(2)}) copy-start(f32[64,64]{0,1:T(8,128)S(1)} %get-tuple-element.19) | copy-start | bytes 49156
  282.0 740.9 %all-to-all-start = ((f32[2,8,4096,128]{3,1,0,2:T(8,128)}), f32[2,8,4096,128]{3,1,0,2:T(8,128)}, u32[]{:S(2)}, u32[]{:S(2)}) async-start(f32[2,8,4096,128]{3,1,0,2:T(8,128)} %copy.37), calls=%async_computation | async-start | bytes 67108864 | tf_op jit(solution)/shard_map/all_to_all | solution.py:81
  1098.2 57.5 %copy-start.1 = (f32[64,64]{0,1:T(8,128)S(1)}, f32[64,64]{0,1:T(8,128)}, u32[]{:S(2)}) copy-start(f32[64,64]{0,1:T(8,128)} %copy-done) | copy-start | bytes 49156
  1098.2 57.5 %copy-start.3 = (f32[64,64]{0,1:T(8,128)S(1)}, f32[64,64]{0,1:T(8,128)}, u32[]{:S(2)}) copy-start(f32[64,64]{0,1:T(8,128)} %copy-done.2) | copy-start | bytes 49156
where the time goes:
time: 1350 us; the launch traced here: 1340 us
  waiting for transfers between devices  734 us (54%)
  matrix products  246 us (18%)
  local copies, waits for them, and re-layouts  219 us (16%)
  other arithmetic  129 us (10%)
    all_to_all x1, waiting for transfers between devices, redistribute(): lax.all_to_all(spectrum, 'pa', split_axis=2, concat_axis=3, tiled=True)  734 us
    dot_general x2, matrix products, transform_last(): jnp.einsum('cdki,dfmij->cfmkj', block_matrix(first_size), tiled, precisio...  120 us
    unnamed x12, local copies, waits for them, and re-layouts  69.8 us
    dot_general x1, matrix products, transform_last(): jnp.einsum('cdlj,dfmkj->cflkm', block_matrix(second_size), turned, precis...  63.2 us
    dot_general x1, matrix products, transform_last(): jnp.einsum('cdlj,dfmkj->cfmlk', block_matrix(second_size), turned, precis...  63.2 us
    slice x3, local copies, waits for them, and re-layouts, body(): return (finished[0], finished[1])  46.5 us
    sub x2, other arithmetic, transform_last(): section_one[0] * twiddle_real - section_one[1] * twiddle_imag  45.7 us
    mul x2, other arithmetic, body(): columns = cancel_along(padded, 3) * col_window  44.3 us
  transfers between devices with their start and end apart: 1, of which 1 were waited for; matrix products, arithmetic and copies ran while one was open for 0% of the time, Pallas kernels for 0%

commit v1 on v0

--- a/solution.py
+++ b/solution.py
@@ -48,7 +48,7 @@
         "cdki,dfmij->cfmkj",
         block_matrix(first_size),
         tiled,
-        precision=lax.Precision.HIGHEST,
+        precision=lax.Precision.HIGH,
         preferred_element_type=jnp.float32,
     )
     twiddle_real, twiddle_imag = twiddle(first_size, second_size, length)
@@ -63,7 +63,7 @@
             "cdlj,dfmkj->cflkm",
             block_matrix(second_size),
             turned,
-            precision=lax.Precision.HIGHEST,
+            precision=lax.Precision.HIGH,
             preferred_element_type=jnp.float32,
         )
         return section_two.reshape(planes, frame_count, length, middle)
@@ -71,25 +71,61 @@
         "cdlj,dfmkj->cfmlk",
         block_matrix(second_size),
         turned,
-        precision=lax.Precision.HIGHEST,
+        precision=lax.Precision.HIGH,
         preferred_element_type=jnp.float32,
     )
     return section_two.reshape(planes, frame_count, middle, length)
 
 
-def redistribute(spectrum):
-    return lax.all_to_all(spectrum, "pa", split_axis=2, concat_axis=3, tiled=True)
+def redistribute(blocks):
+    return lax.all_to_all(blocks, "pa", split_axis=0, concat_axis=0, tiled=True)
+
+
+def first_half(parts, col_window):
+    spectrum = transform_last(jnp.stack(parts) * col_window, True)
+    planes, frames, length, rows = spectrum.shape
+    devices = lax.axis_size("pa")
+    blocks = spectrum.reshape(planes, frames, devices, length // devices, rows)
+    return jnp.transpose(blocks, (2, 0, 1, 3, 4))
+
+
+def second_half(blocks, col_window):
+    devices, planes, frames, kept, rows = blocks.shape
+    length = devices * rows
+    columns = jnp.transpose(blocks, (1, 2, 3, 0, 4)).reshape(planes, frames, kept, length)
+    padded = jnp.pad(columns, ((0, 0), (0, 0), (0, 0), (2, 0)))
+    columns = cancel_along(padded, 3) * col_window
+    return transform_last(columns, False) * (1.0 / length)
 
 
 def body(image_real, image_imag):
     frame_count, row_count, length = image_real.shape
-    stacked = jnp.stack([image_real, image_imag])
     col_window = hamming(0, length, length)
-    columns = redistribute(transform_last(stacked * col_window, True))
-    padded = jnp.pad(columns, ((0, 0), (0, 0), (0, 0), (2, 0)))
-    columns = cancel_along(padded, 3) * col_window
-    finished = transform_last(columns, False) * (1.0 / length)
-    return (finished[0], finished[1])
+    pieces = [
+        (image_real[frame : frame + 1], image_imag[frame : frame + 1])
+        for frame in range(frame_count)
+    ]
+    ready = first_half(pieces[0], col_window)
+    ready, following_piece = lax.optimization_barrier((ready, pieces[min(1, frame_count - 1)]))
+    out_real = jnp.zeros((frame_count, length // lax.axis_size("pa"), length), jnp.float32)
+    out_imag = jnp.zeros_like(out_real)
+    arrived = None
+    for frame in range(frame_count):
+        moving = redistribute(ready)
+        following = ready
+        if frame + 1 < frame_count:
+            following = first_half(following_piece, col_window)
+        if arrived is not None:
+            finished = second_half(arrived, col_window)
+            out_real = lax.dynamic_update_slice(out_real, finished[0], (frame - 1, 0, 0))
+            out_imag = lax.dynamic_update_slice(out_imag, finished[1], (frame - 1, 0, 0))
+        arrived, ready, following_piece, out_real, out_imag = lax.optimization_barrier(
+            (moving, following, pieces[min(frame + 2, frame_count - 1)], out_real, out_imag)
+        )
+    finished = second_half(arrived, col_window)
+    out_real = lax.dynamic_update_slice(out_real, finished[0], (frame_count - 1, 0, 0))
+    out_imag = lax.dynamic_update_slice(out_imag, finished[1], (frame_count - 1, 0, 0))
+    return (out_real, out_imag)
 
 
 def solution(mesh):

time: 1350 us -> 928 us (0.69)
  waiting for transfers between devices: 734 us -> 304 us
  local copies, waits for them, and re-layouts: 219 us -> 340 us
  matrix products: 246 us -> 134 us
  starting transfers between devices: 6.84 us -> 51.5 us
  other arithmetic: 129 us -> 85.1 us
    all_to_all x1 -> x8, waiting for transfers between devices: 734 us -> 304 us  [redistribute(): return lax.all_to_all(blocks, 'pa', split_axis=0, concat_axis=0, tiled=True)]
    optimization_barrier x0 -> x25, local copies, waits for them, and re-layouts: none -> 89.1 us  [the longest x22 80.9 us: body(): lax.optimization_barrier((moving, following, pieces[min(frame + 2, frame_...]
    dot_general x2 -> x16, matrix products: 120 us -> 66.9 us  [transform_last(): jnp.einsum('cdki,dfmij->cfmkj', block_matrix(first_size), tiled, precisio...]
    unnamed x12 -> x49, local copies, waits for them, and re-layouts: 69.8 us -> 24.8 us
    all_to_all x1 -> x8, starting transfers between devices: 6.84 us -> 51.5 us  [redistribute(): return lax.all_to_all(blocks, 'pa', split_axis=0, concat_axis=0, tiled=True)]
    slice x3 -> x26, local copies, waits for them, and re-layouts: 46.5 us -> 91.1 us  [the longest x16 34.5 us: body(): finished[1]]
    reshape x1 -> x0, local copies, waits for them, and re-layouts: 42.9 us -> none  [transform_last(): return section_two.reshape(planes, frame_count, length, middle)]
    squeeze x0 -> x16, local copies, waits for them, and re-layouts: none -> 41.6 us  [the longest x8 25 us: body(): finished[0]]
  transfers between devices with their start and end apart: 1 -> 8, of which waited for: 1 -> 8; matrix products, arithmetic and copies ran while one was open for 0% -> 47% of each run, Pallas kernels for 0% -> 0%
where the time goes in v1:
time: 928 us; the launch traced here: 917 us
  local copies, waits for them, and re-layouts  340 us (37%)
  waiting for transfers between devices  304 us (33%)
  matrix products  134 us (14%)
  other arithmetic  85.1 us (9%)
  starting transfers between devices  51.5 us (6%)
    all_to_all x8, waiting for transfers between devices, redistribute(): return lax.all_to_all(blocks, 'pa', split_axis=0, concat_axis=0, tiled=True)  304 us
    optimization_barrier x22, local copies, waits for them, and re-layouts, body(): lax.optimization_barrier((moving, following, pieces[min(frame + 2, frame_...  80.9 us
    dot_general x16, matrix products, transform_last(): jnp.einsum('cdki,dfmij->cfmkj', block_matrix(first_size), tiled, precisio...  66.9 us
    all_to_all x8, starting transfers between devices, redistribute(): return lax.all_to_all(blocks, 'pa', split_axis=0, concat_axis=0, tiled=True)  51.5 us
    slice x16, local copies, waits for them, and re-layouts, body(): finished[1]  34.5 us
    dot_general x8, matrix products, transform_last(): jnp.einsum('cdlj,dfmkj->cfmlk', block_matrix(second_size), turned, precis...  33.4 us
    transpose x8, local copies, waits for them, and re-layouts, transform_last(): jnp.einsum('cdlj,dfmkj->cflkm', block_matrix(second_size), turned, precis...  33.4 us
    dot_general x8, matrix products, transform_last(): jnp.einsum('cdlj,dfmkj->cflkm', block_matrix(second_size), turned, precis...  33.4 us
  transfers between devices with their start and end apart: 8, of which 8 were waited for; matrix products, arithmetic and copies ran while one was open for 47% of the time, Pallas kernels for 0%

profile of v1, /device:TPU:5, one launch (start us, length us, event | category | flops | bytes accessed | tf_op | source)
XLA Modules:
  0.0 916.6 jit_solution(15814846540736259981)
XLA Ops:
  1.2 11.4 %fusion.186 = (f32[1,128,4096]{2,1,0:T(8,128)}, f32[1,128,4096]{2,1,0:T(8,128)}, f32[1,128,4096]{2,1,0:T(8,128)}, f32[1,128,4096]{2,1,0:T(8,128)S(1)}, f32[1,128...) fusion(f32[8,128,4096]{2,1,0:T(8,128)} %param.2), kind=kLoop, calls=%fused_computation.221 | loop fusion | bytes 33554432 | tf_op jit(solution)/shard_map/slice | solution.py:105
  18.5 12.1 %fusion.185 = (f32[1,128,4096]{2,1,0:T(8,128)}, f32[1,128,4096]{2,1,0:T(8,128)}, f32[1,128,4096]{2,1,0:T(8,128)}, f32[1,128,4096]{2,1,0:T(8,128)}, f32[1,128,409...) fusion(f32[8,128,4096]{2,1,0:T(8,128)} %param.3), kind=kLoop, calls=%fused_computation.220 | loop fusion | bytes 33554432 | tf_op jit(solution)/shard_map/slice | solution.py:105
  54.4 6.8 all-to-all-start
  84.6 68.8 %all-to-all-done = f32[32,2,1,128,128]{4,3,1,2,0:T(8,128)} async-done(((f32[32,2,1,128,128]{4,3,1,2,0:T(8,128)}), f32[32,2,1,128,128]{4,3,1,2,0:T(8,128)}, u32[]{:S(2)}, u32[]{:S(2)}) %all-to-all-start) | async-done | bytes 4194336 | tf_op jit(solution)/shard_map/all_to_all | solution.py:81
  158.2 6.6 all-to-all-start.1
  170.7 5.6 copy.151
  222.3 8.3 broadcast.610
  230.6 11.9 %copy.509 = f32[8,128,4096]{2,1,0:T(8,128)} copy(f32[8,128,4096]{2,1,0:T(8,128)} %broadcast.610) | data formatting | bytes 33554432
  246.2 10.9 %all-to-all-done.1 = f32[32,2,1,128,128]{4,3,1,2,0:T(8,128)} async-done(((f32[32,2,1,128,128]{4,3,1,2,0:T(8,128)}), f32[32,2,1,128,128]{4,3,1,2,0:T(8,128)}, u32[]{:S(2)}, u32[]{:S(2)}) %all-to-all-start.1) | async-done | bytes 4194336 | tf_op jit(solution)/shard_map/all_to_all | solution.py:81
  261.8 6.4 all-to-all-start.2
  273.0 5.7 copy.164
  327.2 33.3 %all-to-all-done.2 = f32[32,2,1,128,128]{4,3,1,2,0:T(8,128)} async-done(((f32[32,2,1,128,128]{4,3,1,2,0:T(8,128)}), f32[32,2,1,128,128]{4,3,1,2,0:T(8,128)}, u32[]{:S(2)}, u32[]{:S(2)}) %all-to-all-start.2) | async-done | bytes 4194336 | tf_op jit(solution)/shard_map/all_to_all | solution.py:81
  365.3 6.4 all-to-all-start.3
  376.4 5.7 copy.177
  430.7 33.2 %all-to-all-done.3 = f32[32,2,1,128,128]{4,3,1,2,0:T(8,128)} async-done(((f32[32,2,1,128,128]{4,3,1,2,0:T(8,128)}), f32[32,2,1,128,128]{4,3,1,2,0:T(8,128)}, u32[]{:S(2)}, u32[]{:S(2)}) %all-to-all-start.3) | async-done | bytes 4194336 | tf_op jit(solution)/shard_map/all_to_all | solution.py:81
  463.9 4.7 copy.184
  468.7 6.3 all-to-all-start.4
  479.9 5.7 copy.190
  534.0 33.3 %all-to-all-done.4 = f32[32,2,1,128,128]{4,3,1,2,0:T(8,128)} async-done(((f32[32,2,1,128,128]{4,3,1,2,0:T(8,128)}), f32[32,2,1,128,128]{4,3,1,2,0:T(8,128)}, u32[]{:S(2)}, u32[]{:S(2)}) %all-to-all-start.4) | async-done | bytes 4194336 | tf_op jit(solution)/shard_map/all_to_all | solution.py:81
  567.3 4.7 copy.197
  572.1 6.3 all-to-all-start.5
  583.2 5.7 copy.203
  637.5 33.2 %all-to-all-done.5 = f32[32,2,1,128,128]{4,3,1,2,0:T(8,128)} async-done(((f32[32,2,1,128,128]{4,3,1,2,0:T(8,128)}), f32[32,2,1,128,128]{4,3,1,2,0:T(8,128)}, u32[]{:S(2)}, u32[]{:S(2)}) %all-to-all-start.5) | async-done | bytes 4194336 | tf_op jit(solution)/shard_map/all_to_all | solution.py:81
  675.4 6.3 all-to-all-start.6
  681.8 5.7 copy.214
  735.9 38.1 %all-to-all-done.6 = f32[32,2,1,128,128]{4,3,1,2,0:T(8,128)} async-done(((f32[32,2,1,128,128]{4,3,1,2,0:T(8,128)}), f32[32,2,1,128,128]{4,3,1,2,0:T(8,128)}, u32[]{:S(2)}, u32[]{:S(2)}) %all-to-all-start.6) | async-done | bytes 4194336 | tf_op jit(solution)/shard_map/all_to_all | solution.py:81
  778.8 6.3 all-to-all-start.7
  785.1 5.6 copy.222
  790.7 5.4 add_multiply_fusion.1
  823.9 53.5 %all-to-all-done.7 = f32[32,2,1,128,128]{4,3,1,2,0:T(8,128)} async-done(((f32[32,2,1,128,128]{4,3,1,2,0:T(8,128)}), f32[32,2,1,128,128]{4,3,1,2,0:T(8,128)}, u32[]{:S(2)}, u32[]{:S(2)}) %all-to-all-start.7) | async-done | bytes 4194336 | tf_op jit(solution)/shard_map/all_to_all | solution.py:81
  877.4 5.7 copy.229
  883.1 5.4 add_multiply_fusion
  (210 shorter events, 449.3 us)
Async XLA Ops:
  54.4 99.1 %all-to-all-start = ((f32[32,2,1,128,128]{4,3,1,2,0:T(8,128)}), f32[32,2,1,128,128]{4,3,1,2,0:T(8,128)}, u32[]{:S(2)}, u32[]{:S(2)}) async-start(f32[32,2,1,128,128]{4,3,1,2,0:T(8,128)} %copy.139), calls=%async_computation | async-start | bytes 8388608 | tf_op jit(solution)/shard_map/all_to_all | solution.py:81
  158.2 98.9 %all-to-all-start.1 = ((f32[32,2,1,128,128]{4,3,1,2,0:T(8,128)}), f32[32,2,1,128,128]{4,3,1,2,0:T(8,128)}, u32[]{:S(2)}, u32[]{:S(2)}) async-start(f32[32,2,1,128,128]{4,3,1,2,0:T(8,128)} %copy.145), calls=%async_computation.1 | async-start | bytes 8388608 | tf_op jit(solution)/shard_map/all_to_all | solution.py:81
  178.9 4.2 copy-start.1
  230.6 11.9 %copy-start.9 = (f32[1,128,4096]{2,1,0:T(8,128)S(1)}, f32[1,128,4096]{2,1,0:T(8,128)}, u32[]{:S(2)}) copy-start(f32[1,128,4096]{2,1,0:T(8,128)} %copy.157) | copy-start | bytes 6291460
  242.4 2.3 copy-start.10
  261.8 98.7 %all-to-all-start.2 = ((f32[32,2,1,128,128]{4,3,1,2,0:T(8,128)}), f32[32,2,1,128,128]{4,3,1,2,0:T(8,128)}, u32[]{:S(2)}, u32[]{:S(2)}) async-start(f32[32,2,1,128,128]{4,3,1,2,0:T(8,128)} %copy.158), calls=%async_computation.2 | async-start | bytes 8388608 | tf_op jit(solution)/shard_map/all_to_all | solution.py:81
  272.9 5.7 copy-start.18
  280.7 4.2 copy-start.2
  323.4 2.3 copy-start.11
  365.3 6.4 copy-start.8
  365.3 98.7 %all-to-all-start.3 = ((f32[32,2,1,128,128]{4,3,1,2,0:T(8,128)}), f32[32,2,1,128,128]{4,3,1,2,0:T(8,128)}, u32[]{:S(2)}, u32[]{:S(2)}) async-start(f32[32,2,1,128,128]{4,3,1,2,0:T(8,128)} %copy.171), calls=%async_computation.3 | async-start | bytes 8388608 | tf_op jit(solution)/shard_map/all_to_all | solution.py:81
  376.4 5.7 copy-start.20
  384.1 4.2 copy-start.3
  426.9 2.3 copy-start.12
  468.7 6.3 copy-start.7
  468.7 98.6 %all-to-all-start.4 = ((f32[32,2,1,128,128]{4,3,1,2,0:T(8,128)}), f32[32,2,1,128,128]{4,3,1,2,0:T(8,128)}, u32[]{:S(2)}, u32[]{:S(2)}) async-start(f32[32,2,1,128,128]{4,3,1,2,0:T(8,128)} %copy.184), calls=%async_computation.4 | async-start | bytes 8388608 | tf_op jit(solution)/shard_map/all_to_all | solution.py:81
  479.9 5.7 copy-start.21
  487.7 4.2 copy-start.4
  530.2 2.3 copy-start.13
  572.1 6.3 copy-start.6
  572.1 98.6 %all-to-all-start.5 = ((f32[32,2,1,128,128]{4,3,1,2,0:T(8,128)}), f32[32,2,1,128,128]{4,3,1,2,0:T(8,128)}, u32[]{:S(2)}, u32[]{:S(2)}) async-start(f32[32,2,1,128,128]{4,3,1,2,0:T(8,128)} %copy.197), calls=%async_computation.5 | async-start | bytes 8388608 | tf_op jit(solution)/shard_map/all_to_all | solution.py:81
  583.2 5.7 copy-start.19
  591.0 4.2 copy-start.5
  633.7 2.3 copy-start.14
  675.4 98.6 %all-to-all-start.6 = ((f32[32,2,1,128,128]{4,3,1,2,0:T(8,128)}), f32[32,2,1,128,128]{4,3,1,2,0:T(8,128)}, u32[]{:S(2)}, u32[]{:S(2)}) async-start(f32[32,2,1,128,128]{4,3,1,2,0:T(8,128)} %copy.210), calls=%async_computation.6 | async-start | bytes 8388608 | tf_op jit(solution)/shard_map/all_to_all | solution.py:81
  681.8 5.8 copy-start.22
  689.6 4.2 copy-start
  732.1 2.3 copy-start.15
  778.8 98.6 %all-to-all-start.7 = ((f32[32,2,1,128,128]{4,3,1,2,0:T(8,128)}), f32[32,2,1,128,128]{4,3,1,2,0:T(8,128)}, u32[]{:S(2)}, u32[]{:S(2)}) async-start(f32[32,2,1,128,128]{4,3,1,2,0:T(8,128)} %copy.221), calls=%async_computation.7 | async-start | bytes 8388608 | tf_op jit(solution)/shard_map/all_to_all | solution.py:81
  820.1 2.3 copy-start.16
  912.6 2.3 copy-start.17
